TPU v7x, 32 devices: a whole 2x2x4 slice. The times are simulated.
32 devices in a mesh: pop: 8 (over z, x), mp: 4 (over y, core).
Axes of the slice: x: 2, y: 2, z: 4, core: 2. Of those that a mesh axis runs over, the one named last changes fastest.
Arguments:
- tokens: bfloat16 [256, 3584], replicated, may hold values from -60 to 60
- target: bfloat16 [256, 3584], P(None, 'mp'), may hold values from -6 to 6
- w_query: bfloat16 [3584, 3584], P('pop', 'mp'), may hold values from -0.09375 to 0.09375
- w_key: bfloat16 [3584, 512], P(None, 'mp'), may hold values from -0.09375 to 0.09375
- w_value: bfloat16 [3584, 512], P(None, 'mp'), may hold values from -0.09375 to 0.09375
- w_out: bfloat16 [3584, 3584], P('mp', 'pop'), may hold values from -0.09375 to 0.09375
- query_left_factors: bfloat16 [8, 3584, 4], P('pop'), may hold values from -0.09375 to 0.09375
- query_right_factors: bfloat16 [8, 4, 3584], P('pop', None, 'mp'), may hold values from -6 to 6
- o_left: bfloat16 [8, 3584, 4], P('pop', 'mp'), may hold values from -0.09375 to 0.09375
- o_right: bfloat16 [8, 4, 3584], P('pop'), may hold values from -6 to 6
- member_ids: int32 [8], P('pop'), may hold values from 0 to 7, each once
Outputs:
- grad_query: float32 [3584, 3584], P('pop', 'mp')
- grad_out: float32 [3584, 3584], P('mp', 'pop')
- fitness: float32 [8], P('pop')
Inputs may be any that keep to these rules, and one draw needn't show every extreme that they name: `member_ids`: every number from 0 to 7 appears once.
All inputs are finite; a program needn't handle non-finite values.
Results may differ from a plain program's by a relative error of at most 0.005.
Values may be sent and summed in bfloat16 or wider, within the bound.
A program may use at most 64 MiB of HBM per device.

v0:
```python
import math
import jax
import jax.numpy as jnp
from jax import lax
from jax.sharding import PartitionSpec as P

D = 3584
HEADS = 28
KV_HEADS = 4
HEAD_DIM = 128
RANK = 4
noise_scale = 0.5
rope_base = 1000000.0
spread_floor = 0.001


def tables(count, head_size):
    position = jnp.arange(count, dtype=jnp.float32)
    index = jnp.arange(head_size // 2, dtype=jnp.float32)
    freq = jnp.exp(-math.log(rope_base) * 2.0 * index / head_size)
    angle = position[:, None] * freq[None, :]
    return (jnp.cos(angle)[:, None, :], jnp.sin(angle)[:, None, :])


def rotate(field, cosine_table, sine):
    half = field.shape[-1] // 2
    first = field[..., :half]
    second = field[..., half:]
    return jnp.concatenate(
        [first * cosine_table - second * sine, second * cosine_table + first * sine], axis=-1
    )


def per_device(
    tokens,
    target,
    w_query,
    w_key,
    w_value,
    w_out,
    query_left_factors,
    query_right_factors,
    o_left,
    o_right,
    member_ids,
):
    tok = tokens.shape[0]
    local_feats = w_query.shape[1]
    local_kv = w_key.shape[1] // HEAD_DIM
    group = HEADS // KV_HEADS
    local_heads = local_kv * group
    slots = query_left_factors.shape[0]
    scale = HEAD_DIM ** (-0.5)
    cosine_table, sine = tables(tok, HEAD_DIM)
    base = jnp.dot(
        tokens,
        lax.all_gather(w_query, "pop", axis=0, tiled=True),
        preferred_element_type=jnp.float32,
    )
    keys = rotate(
        jnp.dot(tokens, w_key, preferred_element_type=jnp.float32).reshape(tok, local_kv, HEAD_DIM),
        cosine_table,
        sine,
    ).astype(jnp.bfloat16)
    values = (
        jnp.dot(tokens, w_value, preferred_element_type=jnp.float32)
        .astype(jnp.bfloat16)
        .reshape(tok, local_kv, HEAD_DIM)
    )
    signs = (1 - 2 * (member_ids % 2)).astype(jnp.float32)
    factor = noise_scale * signs[:, None, None]
    lowrank_product = jnp.einsum(
        "td,mdr->mtr", tokens, query_left_factors, preferred_element_type=jnp.float32
    ).astype(jnp.bfloat16)
    query = base[None] + factor * jnp.einsum(
        "olj,ojv->olv", lowrank_product, query_right_factors, preferred_element_type=jnp.float32
    )
    query = rotate(
        query.reshape(slots, tok, local_heads, HEAD_DIM), cosine_table[None], sine[None]
    ).astype(jnp.bfloat16)
    query = query.reshape(slots, tok, local_kv, group, HEAD_DIM)
    scores = jnp.einsum("mtkgd,skd->mkgts", query, keys, preferred_element_type=jnp.float32) * scale
    causal = jnp.arange(tok)[:, None] >= jnp.arange(tok)[None, :]
    scores = jnp.where(causal, scores, -1e30)
    probs = jax.nn.softmax(scores, axis=-1).astype(jnp.bfloat16)
    mixed = (
        jnp.einsum("mkgts,skd->mtkgd", probs, values, preferred_element_type=jnp.float32)
        .astype(jnp.bfloat16)
        .reshape(slots, tok, local_feats)
    )
    low_out = jnp.einsum("mtf,mfr->mtr", mixed, o_left, preferred_element_type=jnp.float32)
    right_full = o_right.astype(jnp.float32)
    part = jnp.einsum(
        "mtf,fe->mte",
        mixed,
        lax.all_gather(w_out, "pop", axis=1, tiled=True),
        preferred_element_type=jnp.float32,
    )
    term = part + factor * jnp.einsum(
        "mtr,mre->mte", low_out, right_full, precision=lax.Precision.HIGHEST
    )
    output = lax.psum_scatter(
        term.astype(jnp.bfloat16), "mp", scatter_dimension=2, tiled=True
    ).astype(jnp.float32)
    diff = output - target.astype(jnp.float32)[None]
    errors = lax.psum(jnp.sum(diff * diff, axis=(1, 2)), "mp")
    fitness = -(errors / (tok * D))
    count = slots * lax.axis_size("pop")
    mean = lax.psum(jnp.sum(fitness), "pop") / count
    spread = lax.psum(jnp.sum((fitness - mean) * (fitness - mean)), "pop") / count
    weight = signs * (fitness - mean) / jnp.sqrt(spread + spread_floor)
    every_weight = lax.all_gather(weight, "pop", axis=0, tiled=True)
    right_factors_gathered, left_all = (
        lax.all_gather(query_right_factors, "pop", axis=0, tiled=True),
        lax.all_gather(o_left, "pop", axis=0, tiled=True),
    )
    rows_q = lax.all_to_all(query_left_factors, "pop", split_axis=1, concat_axis=0, tiled=True)
    cols_o = lax.all_to_all(o_right, "pop", split_axis=2, concat_axis=0, tiled=True)
    whole_population = rows_q.shape[0]
    left_q = jnp.transpose(
        rows_q.astype(jnp.float32) * every_weight[:, None, None], (1, 0, 2)
    ).reshape(rows_q.shape[1], whole_population * RANK)
    right_q = right_factors_gathered.astype(jnp.float32).reshape(
        whole_population * RANK, local_feats
    )
    grad_query = jnp.dot(left_q, right_q, precision=lax.Precision.HIGHEST) / noise_scale
    output_left_factor = jnp.transpose(
        left_all.astype(jnp.float32) * every_weight[:, None, None], (1, 0, 2)
    ).reshape(local_feats, whole_population * RANK)
    right_o = cols_o.astype(jnp.float32).reshape(whole_population * RANK, cols_o.shape[2])
    grad_out = jnp.dot(output_left_factor, right_o, precision=lax.Precision.HIGHEST) / noise_scale
    return (grad_query, grad_out, fitness)


def solution(mesh):
    placed = (
        P(),
        P(None, "mp"),
        P("pop", "mp"),
        P(None, "mp"),
        P(None, "mp"),
        P("mp", "pop"),
        P("pop", None, None),
        P("pop", None, "mp"),
        P("pop", "mp", None),
        P("pop", None, None),
        P("pop"),
    )
    return jax.shard_map(
        per_device,
        mesh=mesh,
        in_specs=placed,
        out_specs=(P("pop", "mp"), P("mp", "pop"), P("pop")),
        check_vma=False,
    )
```

profile of v0, /device:TPU:0, one launch (start us, length us, event | category | flops | bytes accessed | tf_op | source)
XLA Modules:
  0.0 465.0 jit_solution(14919115663158646740)
XLA Ops:
  12.2 101.0 %all-gather.3.cloned.1.call-done = bf16[3584,896]{1,0:T(8,128)(2,1)} async-done(((bf16[448,896]{1,0:T(8,128)(2,1)}), bf16[3584,896]{1,0:T(8,128)(2,1)}) %all-gather.3.cloned.1.call-update) | async-done | bytes 6422544 | tf_op jit(solution)/shard_map/all_gather | solution.py:57
  113.2 4.9 %fusion.37 = f32[256,896]{1,0:T(8,128)S(1)} fusion(bf16[256,3584]{1,0:T(8,128)(2,1)S(1)} %copy-done, bf16[3584,896]{1,0:T(8,128)(2,1)} %all-gather.3.cloned.1.call-done), kind=kOutput, calls=%fused_computation.66 | convolution fusion | flops 1644167168 | bytes 9175040 | tf_op jit(solution)/shard_map/dot_general | solution.py:55
  118.1 2.7 fusion.4
  129.5 2.9 convolution_convert_fusion
  132.5 81.4 %all-gather.5.cloned.1.call-done = bf16[896,3584]{0,1:T(8,128)(2,1)} async-done(((bf16[896,448]{0,1:T(8,128)(2,1)}), bf16[896,3584]{0,1:T(8,128)(2,1)}) %all-gather.5.cloned.1.call-update) | async-done | bytes 6422544 | tf_op jit(solution)/shard_map/all_gather | solution.py:96
  213.9 4.9 %fusion.38 = f32[256,3584]{1,0:T(8,128)S(1)} fusion(bf16[256,896]{0,1:T(8,128)(2,1)S(1)} %bitcast.110, bf16[896,3584]{0,1:T(8,128)(2,1)} %all-gather.5.cloned.1.call-done), kind=kOutput, calls=%fused_computation.67 | convolution fusion | flops 1644167168 | bytes 10551296 | tf_op jit(solution)/shard_map/mtf,fe->mte/dot_general | solution.py:93
  218.9 3.7 fusion.2
  222.6 8.8 %copy.54 = bf16[1,256,3584]{1,0,2:T(2,128)(2,1)} copy(bf16[1,256,3584]{2,1,0:T(8,128)(2,1)} %fusion.2) | data formatting | bytes 3670016
  231.4 3.6 copy.62
  235.0 3.2 copy.46
  238.8 20.8 %reduce.4 = bf16[3584,4]{1,0:T(8,128)(2,1)S(1)} reduce(bf16[3584,1,4]{2,1,0:T(2,128)(2,1)} %bitcast.105, bf16[]{:T(256)} %broadcast.87), dimensions={1}, to_apply=%bitcast.83.reduce_sub_computation | reduce | bytes 57346
  259.6 2.2 reshape.258
  261.8 3.6 all-to-all-start.1
  265.4 3.2 copy.37
  268.6 20.7 %reduce.3 = bf16[3584,4]{1,0:T(8,128)(2,1)S(1)} reduce(bf16[3584,1,4]{2,1,0:T(2,128)(2,1)} %bitcast.106, bf16[]{:T(256)} %broadcast.87), dimensions={1}, to_apply=%bitcast.81.reduce_sub_computation | reduce | bytes 57346
  289.3 2.2 reshape.256
  292.2 5.7 %all-to-all-start = ((bf16[8,2,896]{2,1,0:T(2,128)(2,1)}), bf16[8,2,896]{2,1,0:T(2,128)(2,1)S(1)}, u32[]{:S(2)}, u32[]{:S(2)}) async-start(bf16[8,2,896]{2,1,0:T(2,128)(2,1)} %reshape.256), calls=%async_computation | async-start | bytes 57344 | tf_op jit(solution)/shard_map/all_to_all | solution.py:117
  297.8 31.3 %all_gather.19 = bf16[8,896,4]{1,2,0:T(4,128)(2,1)S(1)} all-gather(bf16[1,896,4]{1,2,0:T(4,128)(2,1)S(1)} %copy-done.8), channel_id=1, replica_groups=mesh['pop'=8,'mp'=4] {'pop'}, dimensions={0}, use_global_device_ids=true | all-gather | bytes 64512 | tf_op jit(solution)/shard_map/all_gather | solution.py:115
  329.1 30.7 %all_gather.18 = bf16[8,4,896]{2,1,0:T(4,128)(2,1)S(1)} all-gather(bf16[1,4,896]{2,1,0:T(4,128)(2,1)S(1)} %copy-done.9), channel_id=1, replica_groups=mesh['pop'=8,'mp'=4] {'pop'}, dimensions={0}, use_global_device_ids=true | all-gather | bytes 64512 | tf_op jit(solution)/shard_map/all_gather | solution.py:114
  359.8 3.3 reshape.259
  363.2 3.6 copy.47
  367.0 3.3 reshape.257
  370.3 4.6 bitcast_convert_fusion
  378.0 1.9 fusion.8
  379.8 6.3 %psum.21 = f32[1]{0:T(128)} all-reduce(f32[1]{0:T(128)} %bitcast.27), channel_id=1, replica_groups=mesh['pop'=8,'mp'=4] {'mp'}, use_global_device_ids=true, to_apply=%region_4.5 | all-reduce | flops 1 | bytes 8 | tf_op jit(solution)/shard_map/psum | solution.py:106
  387.2 21.8 %psum.22 = f32[]{:T(128)} all-reduce(f32[]{:T(128)} %bitcast.28), channel_id=1, replica_groups=mesh['pop'=8,'mp'=4] {'pop'}, use_global_device_ids=true, to_apply=%region_5.6 | all-reduce | flops 1 | bytes 8 | tf_op jit(solution)/shard_map/psum | solution.py:109
  412.1 18.3 %psum.23 = f32[]{:T(128)} all-reduce(f32[]{:T(128)} %bitcast.30), channel_id=1, replica_groups=mesh['pop'=8,'mp'=4] {'pop'}, use_global_device_ids=true, to_apply=%region_6.7 | all-reduce | flops 1 | bytes 8 | tf_op jit(solution)/shard_map/psum | solution.py:110
  431.1 1.9 divide_dynamic-update-slice_fusion
  433.0 2.1 copy.44
  435.2 19.1 %all-reduce = f32[8]{0:T(128)S(1)} all-reduce(f32[8]{0:T(128)S(1)} %divide_dynamic-update-slice_fusion), channel_id=1, replica_groups=mesh['pop'=8,'mp'=4] {'pop'}, use_global_device_ids=true, to_apply=%add | all-reduce | flops 8 | bytes 64
  454.4 2.0 convolution_multiply_fusion.1
  456.4 2.1 bitcast_multiply_fusion
  (55 shorter events, 17.5 us)
Async XLA Ops:
  7.2 2.8 copy-start
  7.2 2.8 copy-start.2
  7.2 106.0 %all-gather.3.cloned.1.call-start = ((), (), s32[]{:S(2)}) async-start(), calls=%async_computation.3 | async-start | bytes 7225344 | tf_op jit(solution)/shard_map/all_gather | solution.py:57
  7.9 206.0 %all-gather.5.cloned.1.call-start = ((), (), s32[]{:S(2)}) async-start(), calls=%async_computation.4 | async-start | bytes 7225344 | tf_op jit(solution)/shard_map/all_gather | solution.py:96
  8.7 366.2 %reduce-scatter.4.cloned.1.call-start = ((), (), s32[]{:S(2)}) async-start(), calls=%async_computation.5 | async-start | bytes 2293760
  12.2 105.9 %copy-start.6 = (bf16[1,3584,4]{1,2,0:T(4,128)(2,1)S(1)}, bf16[1,3584,4]{1,2,0:T(4,128)(2,1)}, u32[]{:S(2)}) copy-start(bf16[1,3584,4]{1,2,0:T(4,128)(2,1)} %param.17) | copy-start | bytes 86020
  12.2 105.9 %copy-start.9 = (bf16[1,4,896]{2,1,0:T(4,128)(2,1)S(1)}, bf16[1,4,896]{2,1,0:T(4,128)(2,1)}, u32[]{:S(2)}) copy-start(bf16[1,4,896]{2,1,0:T(4,128)(2,1)} %param.18) | copy-start | bytes 21508
  125.9 1.4 copy-start.3
  125.9 1.4 copy-start.4
  127.9 1.2 copy-start.1
  129.4 2.9 copy-start.8
  132.5 86.4 %copy-start.5 = (bf16[1,4,3584]{2,1,0:T(4,128)(2,1)S(1)}, bf16[1,4,3584]{2,1,0:T(4,128)(2,1)}, u32[]{:S(2)}) copy-start(bf16[1,4,3584]{2,1,0:T(4,128)(2,1)} %param.20) | copy-start | bytes 86020
  238.8 26.6 %copy-start.7 = (bf16[1,3584,4]{1,2,0:T(4,128)(2,1)S(1)}, bf16[1,3584,4]{1,2,0:T(4,128)(2,1)}, u32[]{:S(2)}) copy-start(bf16[1,3584,4]{1,2,0:T(4,128)(2,1)} %param.17) | copy-start | bytes 86020
  261.8 30.4 %all-to-all-start.1 = ((bf16[8,2,896]{2,1,0:T(2,128)(2,1)}), bf16[8,2,896]{2,1,0:T(2,128)(2,1)S(1)}, u32[]{:S(2)}, u32[]{:S(2)}) async-start(bf16[8,2,896]{2,1,0:T(2,128)(2,1)} %reshape.258), calls=%async_computation.1 | async-start | bytes 57344 | tf_op jit(solution)/shard_map/all_to_all | solution.py:118
  268.6 23.0 %copy-start.10 = (u32[32]{0:T(128)S(1)}, u32[32]{0:T(128)}, u32[]{:S(2)}) copy-start(u32[32]{0:T(128)} %constant.59) | copy-start | bytes 388
  292.2 74.8 %all-to-all-start = ((bf16[8,2,896]{2,1,0:T(2,128)(2,1)}), bf16[8,2,896]{2,1,0:T(2,128)(2,1)S(1)}, u32[]{:S(2)}, u32[]{:S(2)}) async-start(bf16[8,2,896]{2,1,0:T(2,128)(2,1)} %reshape.256), calls=%async_computation | async-start | bytes 57344 | tf_op jit(solution)/shard_map/all_to_all | solution.py:117
Sparse Core Ops, SparseCore 0:
  10.2 103.0 all-gather.2
  115.4 98.4 all-gather.4
  235.2 27.7 reduce-scatter.3
where the time goes:
time: 466 us; the launch traced here: 465 us
  waiting for transfers between devices  184 us (39%)
  blocking collectives  127 us (27%)
  other arithmetic  53.7 us (12%)
  local copies, waits for them, and re-layouts  46.4 us (10%)
  matrix products  24.7 us (5%)
  between operations  19.6 us (4%)
  starting transfers between devices  9.34 us (2%)
    all_gather x1, waiting for transfers between devices, per_device(): lax.all_gather(w_query, 'pop', axis=0, tiled=True)  101 us
    all_gather x1, waiting for transfers between devices, per_device(): lax.all_gather(w_out, 'pop', axis=1, tiled=True)  81.4 us
    unnamed x3, other arithmetic  43.4 us
    unnamed x37, local copies, waits for them, and re-layouts  38 us
    all_gather x1, blocking collectives, per_device(): lax.all_gather(o_left, 'pop', axis=0, tiled=True)  31.3 us
    all_gather x1, blocking collectives, per_device(): lax.all_gather(query_right_factors, 'pop', axis=0, tiled=True)  30.7 us
    psum x1, blocking collectives, per_device(): mean = lax.psum(jnp.sum(fitness), 'pop') / count  21.8 us
    unnamed x1, blocking collectives  19.1 us
  transfers between devices with their start and end apart: 5, of which 2 were waited for; matrix products, arithmetic and copies ran while one was open for 19% of the time, Pallas kernels for 0%

commit v1 on v0

--- a/solution.py
+++ b/solution.py
@@ -12,6 +12,11 @@
 noise_scale = 0.5
 rope_base = 1000000.0
 spread_floor = 0.001
+
+
+def all_by_exchange(shard, axis, dim):
+    sent = jnp.stack([shard] * lax.axis_size(axis))
+    return jnp.concatenate(lax.all_to_all(sent, axis, 0, 0), axis=dim)
 
 
 def tables(count, head_size):
@@ -112,7 +117,7 @@
     every_weight = lax.all_gather(weight, "pop", axis=0, tiled=True)
     right_factors_gathered, left_all = (
         lax.all_gather(query_right_factors, "pop", axis=0, tiled=True),
-        lax.all_gather(o_left, "pop", axis=0, tiled=True),
+        all_by_exchange(o_left, "pop", 0),
     )
     rows_q = lax.all_to_all(query_left_factors, "pop", split_axis=1, concat_axis=0, tiled=True)
     cols_o = lax.all_to_all(o_right, "pop", split_axis=2, concat_axis=0, tiled=True)

time: 466 us -> 443 us (0.951)
  blocking collectives: 127 us -> 97.4 us
  starting transfers between devices: 9.34 us -> 14.7 us
    all_gather x1 -> x0, blocking collectives: 31.3 us -> none  [per_device(): lax.all_gather(o_left, 'pop', axis=0, tiled=True)]
    all_to_all x0 -> x1, starting transfers between devices: none -> 5.39 us  [all_by_exchange(): return jnp.concatenate(lax.all_to_all(sent, axis, 0, 0), axis=dim)]
    unnamed x37 -> x39, local copies, waits for them, and re-layouts: 38 us -> 38.3 us
  transfers between devices with their start and end apart: 5 -> 6, of which waited for: 2 -> 2; matrix products, arithmetic and copies ran while one was open for 19% -> 22% of each run, Pallas kernels for 0% -> 0%
where the time goes in v1:
time: 443 us; the launch traced here: 441 us
  waiting for transfers between devices  184 us (42%)
  blocking collectives  97.4 us (22%)
  other arithmetic  53.8 us (12%)
  local copies, waits for them, and re-layouts  47.3 us (11%)
  matrix products  24.4 us (6%)
  between operations  19.7 us (4%)
  starting transfers between devices  14.7 us (3%)
    all_gather x1, waiting for transfers between devices, per_device(): lax.all_gather(w_query, 'pop', axis=0, tiled=True)  101 us
    all_gather x1, waiting for transfers between devices, per_device(): lax.all_gather(w_out, 'pop', axis=1, tiled=True)  81.4 us
    unnamed x3, other arithmetic  43.5 us
    unnamed x39, local copies, waits for them, and re-layouts  38.3 us
    all_gather x1, blocking collectives, per_device(): lax.all_gather(query_right_factors, 'pop', axis=0, tiled=True)  31.3 us
    psum x1, blocking collectives, per_device(): mean = lax.psum(jnp.sum(fitness), 'pop') / count  22.4 us
    unnamed x1, blocking collectives  19.1 us
    psum x1, blocking collectives, per_device(): lax.psum(jnp.sum((fitness - mean) * (fitness - mean)), 'pop') / count  18.3 us
  transfers between devices with their start and end apart: 6, of which 2 were waited for; matrix products, arithmetic and copies ran while one was open for 22% of the time, Pallas kernels for 0%

profile of v1, /device:TPU:0, one launch (start us, length us, event | category | flops | bytes accessed | tf_op | source)
XLA Modules:
  0.0 441.1 jit_solution(6073753491619328331)
XLA Ops:
  12.2 101.0 %all-gather.3.cloned.1.call-done = bf16[3584,896]{1,0:T(8,128)(2,1)} async-done(((bf16[448,896]{1,0:T(8,128)(2,1)}), bf16[3584,896]{1,0:T(8,128)(2,1)}) %all-gather.3.cloned.1.call-update) | async-done | bytes 6422544 | tf_op jit(solution)/shard_map/all_gather | solution.py:62
  113.2 4.9 %fusion.38 = f32[256,896]{1,0:T(8,128)S(1)} fusion(bf16[256,3584]{1,0:T(8,128)(2,1)S(1)} %copy-done, bf16[3584,896]{1,0:T(8,128)(2,1)} %all-gather.3.cloned.1.call-done), kind=kOutput, calls=%fused_computation.67 | convolution fusion | flops 1644167168 | bytes 9175040 | tf_op jit(solution)/shard_map/dot_general | solution.py:60
  118.1 2.7 fusion.4
  129.8 2.6 convolution_convert_fusion
  132.6 81.4 %all-gather.5.cloned.1.call-done = bf16[896,3584]{0,1:T(8,128)(2,1)} async-done(((bf16[896,448]{0,1:T(8,128)(2,1)}), bf16[896,3584]{0,1:T(8,128)(2,1)}) %all-gather.5.cloned.1.call-update) | async-done | bytes 6422544 | tf_op jit(solution)/shard_map/all_gather | solution.py:101
  213.9 4.9 %fusion.39 = f32[256,3584]{1,0:T(8,128)S(1)} fusion(bf16[256,896]{0,1:T(8,128)(2,1)S(1)} %bitcast.113, bf16[896,3584]{0,1:T(8,128)(2,1)} %all-gather.5.cloned.1.call-done), kind=kOutput, calls=%fused_computation.68 | convolution fusion | flops 1644167168 | bytes 10551296 | tf_op jit(solution)/shard_map/mtf,fe->mte/dot_general | solution.py:98
  218.9 3.7 fusion.2
  222.6 8.8 %copy.55 = bf16[1,256,3584]{1,0,2:T(2,128)(2,1)} copy(bf16[1,256,3584]{2,1,0:T(8,128)(2,1)} %fusion.2) | data formatting | bytes 3670016
  231.4 3.6 copy.63
  235.0 3.2 copy.47
  238.8 20.8 %reduce.4 = bf16[3584,4]{1,0:T(8,128)(2,1)S(1)} reduce(bf16[3584,1,4]{2,1,0:T(2,128)(2,1)} %bitcast.108, bf16[]{:T(256)} %broadcast.90), dimensions={1}, to_apply=%bitcast.86.reduce_sub_computation | reduce | bytes 57346
  259.6 2.2 reshape.265
  261.8 3.6 all-to-all-start.2
  265.4 3.2 copy.38
  268.6 20.7 %reduce.3 = bf16[3584,4]{1,0:T(8,128)(2,1)S(1)} reduce(bf16[3584,1,4]{2,1,0:T(2,128)(2,1)} %bitcast.109, bf16[]{:T(256)} %broadcast.90), dimensions={1}, to_apply=%bitcast.84.reduce_sub_computation | reduce | bytes 57346
  289.3 2.2 reshape.263
  291.5 5.7 %all-to-all-start = ((bf16[8,2,896]{2,1,0:T(2,128)(2,1)}), bf16[8,2,896]{2,1,0:T(2,128)(2,1)S(1)}, u32[]{:S(2)}, u32[]{:S(2)}) async-start(bf16[8,2,896]{2,1,0:T(2,128)(2,1)} %reshape.263), calls=%async_computation | async-start | bytes 57344 | tf_op jit(solution)/shard_map/all_to_all | solution.py:122
  297.8 31.3 %all_gather.15 = bf16[8,4,896]{2,1,0:T(4,128)(2,1)S(1)} all-gather(bf16[1,4,896]{2,1,0:T(4,128)(2,1)S(1)} %copy-done.8), channel_id=1, replica_groups=mesh['pop'=8,'mp'=4] {'pop'}, dimensions={0}, use_global_device_ids=true | all-gather | bytes 64512 | tf_op jit(solution)/shard_map/all_gather | solution.py:119
  329.1 3.3 reshape.266
  332.4 3.6 copy.48
  336.8 5.4 %all-to-all-start.1 = ((bf16[8,1,896,4]{2,3,1,0:T(4,128)(2,1)}), bf16[8,1,896,4]{2,3,1,0:T(4,128)(2,1)S(1)}, u32[]{:S(2)}, u32[]{:S(2)}) async-start(bf16[8,1,896,4]{2,3,1,0:T(4,128)(2,1)} %stack.2), calls=%async_computation.1 | async-start | bytes 114688 | tf_op jit(solution)/shard_map/all_to_all | solution.py:19
  342.2 3.3 reshape.264
  345.5 4.6 %bitcast_convert_fusion = f32[1,3584,4]{2,0,1:T(1,128)} fusion(bf16[3584,1,4]{2,1,0:T(2,128)(2,1)} %reshape.264), kind=kLoop, calls=%fused_computation.66 | loop fusion | flops 14336 | bytes 86016 | tf_op jit(solution)/shard_map/convert_element_type | solution.py:126
  353.2 1.9 fusion.8
  355.1 6.3 %psum.21 = f32[1]{0:T(128)} all-reduce(f32[1]{0:T(128)} %bitcast.27), channel_id=1, replica_groups=mesh['pop'=8,'mp'=4] {'mp'}, use_global_device_ids=true, to_apply=%region_4.5 | all-reduce | flops 1 | bytes 8 | tf_op jit(solution)/shard_map/psum | solution.py:111
  362.6 22.4 %psum.22 = f32[]{:T(128)} all-reduce(f32[]{:T(128)} %bitcast.28), channel_id=1, replica_groups=mesh['pop'=8,'mp'=4] {'pop'}, use_global_device_ids=true, to_apply=%region_5.6 | all-reduce | flops 1 | bytes 8 | tf_op jit(solution)/shard_map/psum | solution.py:114
  388.2 18.3 %psum.23 = f32[]{:T(128)} all-reduce(f32[]{:T(128)} %bitcast.30), channel_id=1, replica_groups=mesh['pop'=8,'mp'=4] {'pop'}, use_global_device_ids=true, to_apply=%region_6.7 | all-reduce | flops 1 | bytes 8 | tf_op jit(solution)/shard_map/psum | solution.py:115
  407.1 2.0 divide_dynamic-update-slice_fusion
  409.2 2.1 copy.45
  411.3 19.1 %all-reduce = f32[8]{0:T(128)S(1)} all-reduce(f32[8]{0:T(128)S(1)} %divide_dynamic-update-slice_fusion), channel_id=1, replica_groups=mesh['pop'=8,'mp'=4] {'pop'}, use_global_device_ids=true, to_apply=%add | all-reduce | flops 8 | bytes 64
  430.6 2.0 convolution_multiply_fusion.1
  432.6 2.1 bitcast_multiply_fusion
  (59 shorter events, 18.4 us)
Async XLA Ops:
  7.2 2.8 copy-start
  7.2 2.8 copy-start.2
  7.2 106.0 %all-gather.3.cloned.1.call-start = ((), (), s32[]{:S(2)}) async-start(), calls=%async_computation.4 | async-start | bytes 7225344 | tf_op jit(solution)/shard_map/all_gather | solution.py:62
  7.9 206.0 %all-gather.5.cloned.1.call-start = ((), (), s32[]{:S(2)}) async-start(), calls=%async_computation.5 | async-start | bytes 7225344 | tf_op jit(solution)/shard_map/all_gather | solution.py:101
  8.7 341.4 %reduce-scatter.4.cloned.1.call-start = ((), (), s32[]{:S(2)}) async-start(), calls=%async_computation.6 | async-start | bytes 2293760
  12.2 106.0 %copy-start.6 = (bf16[1,3584,4]{1,2,0:T(4,128)(2,1)S(1)}, bf16[1,3584,4]{1,2,0:T(4,128)(2,1)}, u32[]{:S(2)}) copy-start(bf16[1,3584,4]{1,2,0:T(4,128)(2,1)} %param.17) | copy-start | bytes 86020
  12.2 106.0 %copy-start.8 = (bf16[1,4,896]{2,1,0:T(4,128)(2,1)S(1)}, bf16[1,4,896]{2,1,0:T(4,128)(2,1)}, u32[]{:S(2)}) copy-start(bf16[1,4,896]{2,1,0:T(4,128)(2,1)} %param.18) | copy-start | bytes 21508
  125.9 1.4 copy-start.3
  125.9 1.4 copy-start.4
  127.9 1.3 copy-start.1
  127.9 1.8 copy-start.10
  129.8 2.6 copy-start.9
  132.5 86.3 %copy-start.5 = (bf16[1,4,3584]{2,1,0:T(4,128)(2,1)S(1)}, bf16[1,4,3584]{2,1,0:T(4,128)(2,1)}, u32[]{:S(2)}) copy-start(bf16[1,4,3584]{2,1,0:T(4,128)(2,1)} %param.20) | copy-start | bytes 86020
  238.8 26.6 %copy-start.7 = (bf16[1,3584,4]{1,2,0:T(4,128)(2,1)S(1)}, bf16[1,3584,4]{1,2,0:T(4,128)(2,1)}, u32[]{:S(2)}) copy-start(bf16[1,3584,4]{1,2,0:T(4,128)(2,1)} %param.17) | copy-start | bytes 86020
  261.8 29.8 %all-to-all-start.2 = ((bf16[8,2,896]{2,1,0:T(2,128)(2,1)}), bf16[8,2,896]{2,1,0:T(2,128)(2,1)S(1)}, u32[]{:S(2)}, u32[]{:S(2)}) async-start(bf16[8,2,896]{2,1,0:T(2,128)(2,1)} %reshape.265), calls=%async_computation.2 | async-start | bytes 57344 | tf_op jit(solution)/shard_map/all_to_all | solution.py:123
  268.6 28.6 %copy-start.11 = (u32[32]{0:T(128)S(1)}, u32[32]{0:T(128)}, u32[]{:S(2)}) copy-start(u32[32]{0:T(128)} %constant.59) | copy-start | bytes 388
  291.5 44.6 %all-to-all-start = ((bf16[8,2,896]{2,1,0:T(2,128)(2,1)}), bf16[8,2,896]{2,1,0:T(2,128)(2,1)S(1)}, u32[]{:S(2)}, u32[]{:S(2)}) async-start(bf16[8,2,896]{2,1,0:T(2,128)(2,1)} %reshape.263), calls=%async_computation | async-start | bytes 57344 | tf_op jit(solution)/shard_map/all_to_all | solution.py:122
  336.8 93.6 %all-to-all-start.1 = ((bf16[8,1,896,4]{2,3,1,0:T(4,128)(2,1)}), bf16[8,1,896,4]{2,3,1,0:T(4,128)(2,1)S(1)}, u32[]{:S(2)}, u32[]{:S(2)}) async-start(bf16[8,1,896,4]{2,3,1,0:T(4,128)(2,1)} %stack.2), calls=%async_computation.1 | async-start | bytes 114688 | tf_op jit(solution)/shard_map/all_to_all | solution.py:19
Sparse Core Ops, SparseCore 0:
  10.2 103.0 all-gather.2
  115.4 98.4 all-gather.4
  235.2 27.7 reduce-scatter.3
